TPU v7x, 32 devices: a whole 2x2x4 slice. The times are simulated.
32 devices in a mesh: seq: 2 (over x), mp: 4 (over y, core), dp: 4 (over z).
Axes of the slice: x: 2, y: 2, z: 4, core: 2. Of those that a mesh axis runs over, the one named last changes fastest.
Arguments:
- tokens: bfloat16 [16384, 2048], P(('dp', 'seq'), 'mp'), parts along dimension 0, may hold values from -6 to 6
- w_query: bfloat16 [2048, 2048], P(None, 'mp'), may hold values from -0.125 to 0.125
- w_key: bfloat16 [2048, 2048], P(None, 'mp'), may hold values from -0.125 to 0.125
- w_value: bfloat16 [2048, 2048], P(None, 'mp'), may hold values from -0.125 to 0.125
- w_gate: bfloat16 [2048, 2048], P(None, 'mp'), may hold values from -0.125 to 0.125
- decay_exponent: int32 [16], P('mp'), may hold values from 5 to 16
- forget: float32 [16384, 16], P(('dp', 'seq'), 'mp'), parts along dimension 0, may hold values from 0 to 0.69
- norm_gain: float32 [2048], replicated, may hold values from 0.1 to 1.9
Outputs:
- retained: bfloat16 [16384, 2048], P(('dp', 'seq', 'mp')), parts along dimension 0
There are 4 independent parts, one for each index of `dp`. A program takes and returns all parts, laid end to end along the dimension named above; an argument that names none is the same for every part. Nothing has to cross between parts.
All inputs are finite; a program needn't handle non-finite values.
Results may differ from a plain program's by a relative error of at most 0.015.
Values may be sent and summed in bfloat16 or wider, within the bound.
A program may use at most 64 MiB of HBM per device.

v0:
```python
import jax
import jax.numpy as jnp
from jax import lax
from jax.sharding import PartitionSpec as P

DH = 128


def carried_in(shard, axis, join, neutral):
    place = lax.axis_index(axis)
    gathered = jax.tree.map(
        lambda a, kind: lax.all_gather(a.astype(kind), axis), shard, (jnp.bfloat16, jnp.bfloat16)
    )
    state = jax.tree.map(lambda a, e: jnp.zeros_like(a) + jnp.asarray(e, a.dtype), shard, neutral)

    def one(hop, state):
        return join(
            state,
            jax.tree.map(
                lambda a, own: lax.dynamic_index_in_dim(a, hop, 0, False).astype(own.dtype),
                gathered,
                shard,
            ),
        )

    return lax.fori_loop(0, place, one, state)


def run_blocks(queries, key_rows, values, logdecay, head_count, head_width):
    seq_rows = queries.shape[0]
    block_rows = 512
    block_count = seq_rows // block_rows

    def shaped(source):
        return source.reshape(block_count, block_rows, head_count, head_width)

    decays = logdecay.reshape(block_count, block_rows, head_count)
    position = lax.broadcasted_iota(jnp.int32, (block_rows, block_rows), 0)
    earlier = lax.broadcasted_iota(jnp.int32, (block_rows, block_rows), 1)
    causal = position >= earlier

    def advance(carried, pieces):
        kv_state, offset = carried
        query_blk, key_blk, value_blk, decay_blk = pieces
        running = jnp.cumsum(decay_blk, axis=0)
        heads_first = running.T
        log_gap = heads_first[:, :, None] - heads_first[:, None, :]
        decay_mask = jnp.where(causal[None], jnp.exp(jnp.where(causal[None], log_gap, 0.0)), 0.0)
        scores = jnp.einsum("tha,sha->hts", query_blk, key_blk, preferred_element_type=jnp.float32)
        scores = (scores * decay_mask).astype(jnp.bfloat16)
        inner = jnp.einsum("hts,shb->thb", scores, value_blk, preferred_element_type=jnp.float32)
        query_float = query_blk.astype(jnp.float32)
        earlier_part = jnp.einsum(
            "tha,hab->thb",
            query_float * jnp.exp(running)[:, :, None],
            kv_state,
            precision=lax.Precision.HIGHEST,
        )
        query_device = query_float * jnp.exp(running + offset[None, :])[:, :, None]
        key_scaled = key_blk.astype(jnp.float32) * jnp.exp(running[-1:] - running)[:, :, None]
        kv_state = jnp.exp(running[-1])[:, None, None] * kv_state + jnp.einsum(
            "sha,shb->hab",
            key_scaled,
            value_blk.astype(jnp.float32),
            precision=lax.Precision.HIGHEST,
        )
        return ((kv_state, offset + running[-1]), (inner + earlier_part, query_device))

    initial = (
        jnp.zeros((head_count, head_width, head_width), jnp.float32),
        jnp.zeros((head_count,), jnp.float32),
    )
    final, outputs = lax.scan(
        advance, initial, (shaped(queries), shaped(key_rows), shaped(values), decays)
    )
    local_part = outputs[0].reshape(seq_rows, head_count, head_width)
    query_device = outputs[1].reshape(seq_rows, head_count, head_width)
    return (local_part, query_device, final[0], final[1])


def combine_states(before, after):
    return (before[0] * after[0], after[0][:, None, None] * before[1] + after[1])


def body(tokens, w_query, w_key, w_value, w_gate, decay_exponent, forget, norm_gain):
    seq_rows = tokens.shape[0]
    local_width = w_query.shape[1]
    head_count = decay_exponent.shape[0]
    head_width = local_width // head_count
    empty = jnp.zeros((seq_rows, local_width), jnp.float32)
    summed = (empty, empty, empty, empty)
    piece = lax.all_gather(tokens, "mp", axis=1, tiled=True)
    results = []
    for weight, partial_value in zip((w_query, w_key, w_value, w_gate), summed):
        results.append(jnp.dot(piece, weight, preferred_element_type=jnp.float32))
    projected = tuple(results)
    queries = projected[0].astype(jnp.bfloat16)
    key_rows = (projected[1] * DH ** (-0.5)).astype(jnp.bfloat16)
    values = projected[2].astype(jnp.bfloat16)
    gate = projected[3].astype(jnp.bfloat16)
    rate = jnp.log1p(-jnp.exp2(-decay_exponent.astype(jnp.float32)))
    logdecay = rate[None, :] - forget
    local_part, query_device, own_state, own_total = run_blocks(
        queries, key_rows, values, logdecay, head_count, head_width
    )
    prefix = carried_in(
        (jnp.exp(own_total), own_state),
        "seq",
        combine_states,
        (jnp.ones_like(own_total), jnp.zeros_like(own_state)),
    )
    incoming = prefix[1]
    from_before = jnp.einsum(
        "tha,hab->thb", query_device, incoming, precision=lax.Precision.HIGHEST
    )
    output = (local_part + from_before).astype(jnp.bfloat16).reshape(seq_rows, local_width)
    moved_output, moved_gate = (
        lax.all_to_all(output, "mp", split_axis=0, concat_axis=1, tiled=True),
        lax.all_to_all(gate, "mp", split_axis=0, concat_axis=1, tiled=True),
    )
    output_float = moved_output.astype(jnp.float32)
    rstd = lax.rsqrt(jnp.mean(output_float * output_float, axis=1) + 1e-06)
    gated = (
        jax.nn.silu(moved_gate.astype(jnp.float32))
        * output_float
        * rstd[:, None]
        * norm_gain[None, :]
    )
    return gated.astype(jnp.bfloat16)


def solution(mesh):
    placed = (
        P(("dp", "seq"), "mp"),
        P(None, "mp"),
        P(None, "mp"),
        P(None, "mp"),
        P(None, "mp"),
        P("mp"),
        P(("dp", "seq"), "mp"),
        P(),
    )
    return jax.shard_map(
        body, mesh=mesh, in_specs=placed, out_specs=P(("dp", "seq", "mp"), None), check_vma=False
    )
```

profile of v0, /device:TPU:11, one launch (start us, length us, event | category | flops | bytes accessed | tf_op | source)
XLA Modules:
  0.0 335.7 jit_solution(5486481289894038509)
XLA Ops:
  6.5 0.7 all-gather.4.cloned.1.call-update
  7.3 1.2 dynamic-slice
  9.2 0.7 negate_log-plus-one_fusion
  9.9 0.8 broadcast_subtract_fusion
  10.7 58.0 %all-gather.4.cloned.1.call-done = bf16[2048,2048]{1,0:T(8,128)(2,1)} async-done(((bf16[2048,512]{1,0:T(8,128)(2,1)}), bf16[2048,2048]{1,0:T(8,128)(2,1)}) %all-gather.4.cloned.1.call-update) | async-done | bytes 8388624 | tf_op jit(solution)/shard_map/all_gather | solution.py:92
  68.7 9.1 %convolution_convert_fusion = bf16[2048,512]{1,0:T(8,128)(2,1)} fusion(bf16[2048,2048]{1,0:T(8,128)(2,1)} %all-gather.4.cloned.1.call-done, bf16[2048,512]{1,0:T(8,128)(2,1)S(1)} %copy-done), kind=kOutput, calls=%fused_computation.48 | convolution fusion | flops 4296015872 | bytes 12582912 | tf_op jit(solution)/shard_map/dot_general | solution.py:95
  77.8 4.0 %reshape.90 = bf16[4,512,4,128]{3,2,1,0:T(4,128)(2,1)} reshape(bf16[2048,512]{1,0:T(8,128)(2,1)} %convolution_convert_fusion) | data formatting | bytes 4194304 | tf_op jit(solution)/shard_map/reshape | solution.py:35
  81.8 8.5 %convolution_convert_fusion.1 = bf16[2048,512]{1,0:T(8,128)(2,1)S(1)} fusion(bf16[2048,2048]{1,0:T(8,128)(2,1)} %all-gather.4.cloned.1.call-done, bf16[2048,512]{1,0:T(8,128)(2,1)} %param.15), kind=kOutput, calls=%fused_computation.49 | convolution fusion | flops 4296015872 | bytes 12582912 | tf_op jit(solution)/shard_map/dot_general | solution.py:95
  90.3 2.1 reshape.89
  92.4 8.5 %multiply_convert_fusion.2 = bf16[2048,512]{1,0:T(8,128)(2,1)S(1)} fusion(bf16[2048,2048]{1,0:T(8,128)(2,1)} %all-gather.4.cloned.1.call-done, bf16[2048,512]{1,0:T(8,128)(2,1)} %param.14), kind=kOutput, calls=%fused_computation.47 | convolution fusion | flops 4297064448 | bytes 12582912 | tf_op jit(solution)/shard_map/dot_general | solution.py:95
  100.9 2.0 reshape.88
  102.9 137.0 %while.31 = (s32[]{:T(128)}, f32[4,128,128]{2,1,0:T(8,128)S(1)}, f32[4]{0:T(128)S(1)}, f32[4,512,4,128]{1,0,3,2:T(4,128)}, f32[4,512,4,128]{3,1,0,2:T(8,128)}, /...) while((s32[]{:T(128)}, f32[4,128,128]{2,1,0:T(8,128)S(1)}, ...), condition=%wide.region_3.4_spmd.clone.clone, body=%wide.region_0.3_spmd.clone.clone.sunk | while | flops 1350045696 | bytes 18760368 | solution.py:73
  102.9 1.2 reduce-window.16
  104.9 1.2 constant_dynamic-slice_fusion.5
  106.2 1.8 constant_dynamic-slice_fusion.6
  108.0 2.0 fusion.48
  109.9 1.4 fusion.49
  111.3 2.4 convolution_add_fusion.2
  113.7 1.1 copy.143
  114.8 21.0 %dynamic_update_slice.15 = f32[4,512,4,128]{1,0,3,2:T(4,128)} dynamic-update-slice(f32[4,512,4,128]{1,0,3,2:T(4,128)} %get-tuple-element.371, f32[1,512,4,128]{1,0,3,2:T(1,128)S(1)} %copy.143, s32[]{:T(128)S(6)} %copy.151, s32[]{:T(128)} %constant.52.clone.1..sunk.1, s32[]{:T(128)} %constant.52.clone.1..sunk.1, s32[]{:T(128)} %constant.52.clone.1..sunk.1) | dynamic-update-slice | bytes 2097156 | tf_op jit(solution)/shard_map/while/body/jit(dynamic_update_index_in_dim)/dynamic_update_slice | solution.py:73
  135.8 1.3 bitcast_dynamic-update-slice_fusion.2
  137.2 1.2 reduce-window.16
  139.2 1.2 constant_dynamic-slice_fusion.5
  140.5 1.8 constant_dynamic-slice_fusion.6
  142.2 2.0 fusion.48
  144.2 1.4 fusion.49
  145.6 2.4 convolution_add_fusion.2
  148.0 1.1 copy.143
  149.0 21.0 %dynamic_update_slice.15 = f32[4,512,4,128]{1,0,3,2:T(4,128)} dynamic-update-slice(f32[4,512,4,128]{1,0,3,2:T(4,128)} %get-tuple-element.371, f32[1,512,4,128]{1,0,3,2:T(1,128)S(1)} %copy.143, s32[]{:T(128)S(6)} %copy.151, s32[]{:T(128)} %constant.52.clone.1..sunk.1, s32[]{:T(128)} %constant.52.clone.1..sunk.1, s32[]{:T(128)} %constant.52.clone.1..sunk.1) | dynamic-update-slice | bytes 2097156 | tf_op jit(solution)/shard_map/while/body/jit(dynamic_update_index_in_dim)/dynamic_update_slice | solution.py:73
  170.1 1.3 bitcast_dynamic-update-slice_fusion.2
  171.4 1.2 reduce-window.16
  173.5 1.2 constant_dynamic-slice_fusion.5
  174.7 1.8 constant_dynamic-slice_fusion.6
  176.5 2.0 fusion.48
  178.5 1.4 fusion.49
  179.8 2.4 convolution_add_fusion.2
  182.2 1.1 copy.143
  183.3 21.0 %dynamic_update_slice.15 = f32[4,512,4,128]{1,0,3,2:T(4,128)} dynamic-update-slice(f32[4,512,4,128]{1,0,3,2:T(4,128)} %get-tuple-element.371, f32[1,512,4,128]{1,0,3,2:T(1,128)S(1)} %copy.143, s32[]{:T(128)S(6)} %copy.151, s32[]{:T(128)} %constant.52.clone.1..sunk.1, s32[]{:T(128)} %constant.52.clone.1..sunk.1, s32[]{:T(128)} %constant.52.clone.1..sunk.1) | dynamic-update-slice | bytes 2097156 | tf_op jit(solution)/shard_map/while/body/jit(dynamic_update_index_in_dim)/dynamic_update_slice | solution.py:73
  204.3 1.3 bitcast_dynamic-update-slice_fusion.2
  205.7 1.2 reduce-window.16
  207.7 1.2 constant_dynamic-slice_fusion.5
  208.9 1.8 constant_dynamic-slice_fusion.6
  210.7 2.0 fusion.48
  212.7 1.4 fusion.49
  214.1 2.4 convolution_add_fusion.2
  216.5 1.1 copy.143
  217.5 21.0 %dynamic_update_slice.15 = f32[4,512,4,128]{1,0,3,2:T(4,128)} dynamic-update-slice(f32[4,512,4,128]{1,0,3,2:T(4,128)} %get-tuple-element.371, f32[1,512,4,128]{1,0,3,2:T(1,128)S(1)} %copy.143, s32[]{:T(128)S(6)} %copy.151, s32[]{:T(128)} %constant.52.clone.1..sunk.1, s32[]{:T(128)} %constant.52.clone.1..sunk.1, s32[]{:T(128)} %constant.52.clone.1..sunk.1) | dynamic-update-slice | bytes 2097156 | tf_op jit(solution)/shard_map/while/body/jit(dynamic_update_index_in_dim)/dynamic_update_slice | solution.py:73
  238.6 1.3 bitcast_dynamic-update-slice_fusion.2
  240.2 9.8 %convolution_convert_fusion.2 = bf16[2048,512]{1,0:T(8,128)(2,1)} fusion(bf16[2048,2048]{1,0:T(8,128)(2,1)} %all-gather.4.cloned.1.call-done, bf16[2048,512]{1,0:T(8,128)(2,1)} %param.16), kind=kOutput, calls=%fused_computation.50 | convolution fusion | flops 4296015872 | bytes 12582912 | tf_op jit(solution)/shard_map/dot_general | solution.py:95
  250.0 4.7 %all-to-all-start = ((bf16[4,512,512]{2,1,0:T(8,128)(2,1)}), bf16[4,512,512]{2,1,0:T(8,128)(2,1)}, u32[]{:S(2)}, u32[]{:S(2)}) async-start(bf16[4,512,512]{2,1,0:T(8,128)(2,1)} %bitcast.2), calls=%async_computation | async-start | bytes 4194304 | tf_op jit(solution)/shard_map/all_to_all | solution.py:119
  254.7 4.2 %all-reduce = bf16[8]{0:T(256)(128)(2,1)S(1)} all-reduce(bf16[8]{0:T(256)(128)(2,1)S(1)} %dynamic-update-slice), channel_id=2, replica_groups=mesh['seq'=2,'mp'=4,'dp'=4] {'seq'}, use_global_device_ids=true, to_apply=%add | all-reduce | flops 8 | bytes 32
  259.0 5.0 %all-gather.1 = bf16[8,128,128]{2,1,0:T(8,128)(2,1)S(1)} all-gather(bf16[4,128,128]{2,1,0:T(8,128)(2,1)S(1)} %convert_element_type.89), channel_id=3, replica_groups=mesh['seq'=2,'mp'=4,'dp'=4] {'seq'}, dimensions={0}, use_global_device_ids=true | all-gather | bytes 393216 | tf_op jit(solution)/shard_map/all_gather | solution.py:12
  264.0 6.1 %reshape.91 = f32[2048,4,128]{0,2,1:T(8,128)} reshape(f32[4,512,4,128]{1,0,3,2:T(4,128)} %get-tuple-element.107) | data formatting | bytes 8388608 | tf_op jit(solution)/shard_map/reshape | solution.py:76
  270.2 8.8 %fusion.24 = bf16[2048,4,128]{0,2,1:T(8,128)(2,1)} fusion(f32[2048,4,128]{0,2,1:T(8,128)} %reshape.91, f32[4,128,128]{2,1,0:T(8,128)S(1)} %get-tuple-element.110, f32[2048,4,128]{2,0,1:T(8,128)} %bitcast.128), kind=kOutput, calls=%fused_computation.43 | convolution fusion | flops 1612709888 | bytes 10747904 | tf_op jit(solution)/shard_map/tha,hab->thb/dot_general | solution.py:113
  279.0 3.3 all_to_all.22
  282.3 1.7 copy.79
  284.1 5.2 %all-to-all-start.1 = ((bf16[4,512,512]{1,2,0:T(8,128)(2,1)}), bf16[4,512,512]{1,2,0:T(8,128)(2,1)S(1)}, u32[]{:S(2)}, u32[]{:S(2)}) async-start(bf16[4,512,512]{1,2,0:T(8,128)(2,1)} %copy.79), calls=%async_computation.1 | async-start | bytes 4194304 | tf_op jit(solution)/shard_map/all_to_all | solution.py:118
  289.2 2.2 convert_bitcast_fusion
  291.4 2.6 copy.94
  294.0 20.0 %all-to-all-done.1 = bf16[4,512,512]{1,2,0:T(8,128)(2,1)S(1)} async-done(((bf16[4,512,512]{1,2,0:T(8,128)(2,1)}), bf16[4,512,512]{1,2,0:T(8,128)(2,1)S(1)}, u32[]{:S(2)}, u32[]{:S(2)}) %all-to-all-start.1) | async-done | bytes 2097184 | tf_op jit(solution)/shard_map/all_to_all | solution.py:118
  313.9 0.5 multiply_reduce_fusion
  314.5 2.6 convert_element_type.105
  317.0 5.4 %copy.80 = f32[512,2048]{1,0:T(8,128)} copy(f32[512,2048]{0,1:T(8,128)} %bitcast.127) | data formatting | bytes 8388608 | tf_op jit(solution)/shard_map/convert_element_type | solution.py:121
  322.5 6.4 %multiply_convert_fusion.1 = bf16[512,2048]{1,0:T(8,128)(2,1)} fusion(f32[512,2048]{1,0:T(8,128)} %copy.80, f32[512,2048]{1,0:T(8,128)} %bitcast.126, f32[2048]{0:T(1024)S(1)} %copy-done.3, f32[512]{0:T(512)S(1)} %add_rsqrt_fusion), kind=kLoop, calls=%fused_computation.45 | loop fusion | flops 8388608 | bytes 10496000 | tf_op jit(solution)/shard_map/convert_element_type | solution.py:129
  (70 shorter events, 3.9 us)
Async XLA Ops:
  6.5 62.2 %copy-start = (bf16[2048,512]{1,0:T(8,128)(2,1)S(1)}, bf16[2048,512]{1,0:T(8,128)(2,1)}, u32[]{:S(2)}) copy-start(bf16[2048,512]{1,0:T(8,128)(2,1)} %param.13) | copy-start | bytes 6291460
  6.5 62.2 %all-gather.4.cloned.1.call-start = ((), (), s32[]{:S(2)}) async-start(), calls=%async_computation.2 | async-start | bytes 10485760 | tf_op jit(solution)/shard_map/all_gather | solution.py:92
  106.2 1.8 copy-start.2
  140.4 1.8 copy-start.2
  174.7 1.8 copy-start.2
  208.9 1.8 copy-start.2
  250.0 34.0 %all-to-all-start = ((bf16[4,512,512]{2,1,0:T(8,128)(2,1)}), bf16[4,512,512]{2,1,0:T(8,128)(2,1)}, u32[]{:S(2)}, u32[]{:S(2)}) async-start(bf16[4,512,512]{2,1,0:T(8,128)(2,1)} %bitcast.2), calls=%async_computation | async-start | bytes 4194304 | tf_op jit(solution)/shard_map/all_to_all | solution.py:119
  284.1 29.9 %all-to-all-start.1 = ((bf16[4,512,512]{1,2,0:T(8,128)(2,1)}), bf16[4,512,512]{1,2,0:T(8,128)(2,1)S(1)}, u32[]{:S(2)}, u32[]{:S(2)}) async-start(bf16[4,512,512]{1,2,0:T(8,128)(2,1)} %copy.79), calls=%async_computation.1 | async-start | bytes 4194304 | tf_op jit(solution)/shard_map/all_to_all | solution.py:118
  317.0 5.4 %copy-start.3 = (f32[2048]{0:T(1024)S(1)}, f32[2048]{0:T(1024)}, u32[]{:S(2)}) copy-start(f32[2048]{0:T(1024)} %param.19) | copy-start | bytes 24580
  322.4 6.4 %copy-start.1 = (bf16[2048,512]{1,0:T(8,128)(2,1)S(1)}, bf16[2048,512]{1,0:T(8,128)(2,1)}, u32[]{:S(2)}) copy-start(bf16[2048,512]{1,0:T(8,128)(2,1)} %param.13) | copy-start | bytes 6291460
Sparse Core Ops, SparseCore 0:
  8.9 59.8 all-gather.3
where the time goes:
time: 341 us; the launch traced here: 336 us
  local copies, waits for them, and re-layouts  131 us (38%)
  waiting for transfers between devices  78.7 us (23%)
  matrix products  67.6 us (20%)
  other arithmetic  25.2 us (7%)
  between operations  14.1 us (4%)
  starting transfers between devices  9.83 us (3%)
  blocking collectives  9.15 us (3%)
    dynamic_update_slice x8, local copies, waits for them, and re-layouts, run_blocks(): lax.scan(advance, initial, (shaped(queries), shaped(key_rows), shaped(val...  88.5 us
    all_gather x1, waiting for transfers between devices, body(): piece = lax.all_gather(tokens, 'mp', axis=1, tiled=True)  58 us
    dot_general x4, matrix products, body(): results.append(jnp.dot(piece, weight, preferred_element_type=jnp.float32))  35.9 us
    all_to_all x1, waiting for transfers between devices, body(): lax.all_to_all(output, 'mp', split_axis=0, concat_axis=1, tiled=True)  20 us
    dynamic_slice x8, local copies, waits for them, and re-layouts, run_blocks(): lax.scan(advance, initial, (shaped(queries), shaped(key_rows), shaped(val...  11.9 us
    dot_general x4, matrix products, advance(): jnp.einsum('sha,shb->hab', key_scaled, value_blk.astype(jnp.float32), pre...  9.56 us
    dot_general x1, matrix products, body(): jnp.einsum('tha,hab->thb', query_device, incoming, precision=lax.Precisio...  8.83 us
    reshape x3, local copies, waits for them, and re-layouts, shaped(): return source.reshape(block_count, block_rows, head_count, head_width)  8.09 us
  transfers between devices with their start and end apart: 3, of which 2 were waited for; matrix products, arithmetic and copies ran while one was open for 7% of the time, Pallas kernels for 0%

commit v1 on v0

v1 whole, which is shorter than its diff:
```python
import functools

import jax
import jax.numpy as jnp
from jax import lax
from jax.experimental import pallas as pl
from jax.experimental.pallas import tpu as pltpu
from jax.sharding import PartitionSpec as P

DH = 128
MESH = pl.DeviceIdType.MESH
F32 = jnp.float32
BF16 = jnp.bfloat16


def contract(a, b, dims):
    return lax.dot_general(a, b, ((dims[0], dims[1]), ((), ())), preferred_element_type=F32)


def kernel(
    n_mp, n_seq, heads, rows,
    tokens, wq, wk, wv, wg, decay, gain, out,
    x, w, local_out, q_in, moved, got, sq_out, sq_got, gates, state, enter, state_out, state_got, offset,
    weight_sem, own_sem, y_send, y_recv, d_send, d_recv, s_send, s_recv, m_send, m_recv, q_send, q_recv,
):
    me = lax.axis_index("mp")
    place = lax.axis_index("seq")
    chips = n_mp // 2
    chip, core = me // 2, me % 2
    partner = chip * 2 + (1 - core)
    seq_rows, width = tokens.shape
    chunks = seq_rows // rows
    own_rows = seq_rows // n_mp
    parts = own_rows // rows
    head_width = width // heads

    weights = [pltpu.make_async_copy(src, w.at[i], weight_sem.at[i]) for i, src in enumerate((wq, wk, wv, wg))]

    def columns(block):
        return pl.ds(pl.multiple_of(block * width, width), width)

    def at_rows(c):
        return pl.ds(pl.multiple_of(c * rows, rows), rows)

    def own_copy(c):
        return pltpu.make_async_copy(tokens.at[at_rows(c), :], x.at[at_rows(c), columns(me)], own_sem.at[c])

    def far(step):
        return lax.rem(chip + step, chips) * 2 + core

    def back(step):
        return lax.rem(chip + chips - step, chips) * 2 + core

    def y_copy(c, step):
        return pltpu.make_async_remote_copy(
            src_ref=tokens.at[at_rows(c), :], dst_ref=x.at[at_rows(c), columns(me)],
            send_sem=y_send.at[c, step], recv_sem=y_recv.at[c, step],
            device_id={"mp": far(step)}, device_id_type=MESH)

    def y_arrival(c, step):
        return pltpu.make_async_remote_copy(
            src_ref=tokens.at[at_rows(c), :], dst_ref=x.at[at_rows(c), columns(back(step))],
            send_sem=y_send.at[c, step], recv_sem=y_recv.at[c, step],
            device_id={"mp": far(step)}, device_id_type=MESH)

    def d_copy(c, step):
        block = me if step == 0 else back(step)
        source = tokens.at[at_rows(c), :] if step == 0 else x.at[at_rows(c), columns(block)]
        return pltpu.make_async_remote_copy(
            src_ref=source, dst_ref=x.at[at_rows(c), columns(block)],
            send_sem=d_send.at[c, step], recv_sem=d_recv.at[c, step],
            device_id={"mp": partner}, device_id_type=MESH)

    def d_arrival(c, step):
        block = partner if step == 0 else lax.rem(chip + chips - step, chips) * 2 + (1 - core)
        there = x.at[at_rows(c), columns(block)]
        return pltpu.make_async_remote_copy(
            src_ref=there, dst_ref=there, send_sem=d_send.at[c, step], recv_sem=d_recv.at[c, step],
            device_id={"mp": partner}, device_id_type=MESH)

    barrier = pltpu.get_barrier_semaphore()
    for other in range(1, n_mp):
        pl.semaphore_signal(barrier, inc=1, device_id={"mp": lax.rem(me + other, n_mp)}, device_id_type=MESH)

    @pl.when(place > 0)
    def _():
        pl.semaphore_signal(barrier, inc=1, device_id={"seq": place - 1}, device_id_type=MESH)

    @pl.when(place < n_seq - 1)
    def _():
        pl.semaphore_signal(barrier, inc=1, device_id={"seq": place + 1}, device_id_type=MESH)

    for i in range(3):
        weights[i].start()
    pl.loop(0, chunks)(lambda c: own_copy(c).start())
    weights[3].start()

    neighbours = jnp.minimum(place, 1) + jnp.minimum(n_seq - 1 - place, 1)
    pl.semaphore_wait(barrier, n_mp - 1 + neighbours)

    @pl.loop(0, chunks)
    def _(c):
        for step in range(1, chips):
            y_copy(c, step).start()
        d_copy(c, 0).start()

    state[...] = jnp.zeros_like(state)
    offset[...] = jnp.zeros_like(offset)
    for i in range(3):
        weights[i].wait()

    later = lax.broadcasted_iota(jnp.int32, (rows, rows), 0)
    earlier = lax.broadcasted_iota(jnp.int32, (rows, rows), 1)
    causal = later >= earlier
    summing = (later <= earlier).astype(F32)

    @pl.loop(0, chunks)
    def _(c):
        here = at_rows(c)
        for step in range(1, chips):
            y_arrival(c, step).wait_recv()
            d_copy(c, step).start()
        own_copy(c).wait()
        running = jnp.dot(decay[:, here], summing, precision=lax.Precision.HIGHEST, preferred_element_type=F32)
        by_row = running.T
        last = running[:, rows - 1 :]
        before = offset[...]
        for step in range(chips):
            d_arrival(c, step).wait_recv()
        piece = x[here, :]
        query = jnp.dot(piece, w[0], preferred_element_type=F32).astype(BF16)
        key = (jnp.dot(piece, w[1], preferred_element_type=F32) * DH ** (-0.5)).astype(BF16)
        value = jnp.dot(piece, w[2], preferred_element_type=F32).astype(BF16)
        for h in range(heads):
            part = slice(h * head_width, (h + 1) * head_width)
            q, k, v = query[:, part], key[:, part], value[:, part]
            col = by_row[:, h : h + 1]
            mask = jnp.exp(jnp.where(causal, col - running[h : h + 1, :], -1e30))
            scores = (contract(q, k, ((1,), (1,))) * mask).astype(BF16)
            grown = state[h]
            qf = q.astype(F32)
            carried = jnp.dot((qf * jnp.exp(col)).astype(BF16), grown.astype(BF16), preferred_element_type=F32)
            local_out[here, part] = jnp.dot(scores, v, preferred_element_type=F32) + carried
            q_in[here, part] = (qf * jnp.exp(col + before[h : h + 1, 0:1])).astype(BF16)
            faded = (k.astype(F32) * jnp.exp(last[h : h + 1, :] - col)).astype(BF16)
            state[h] = jnp.exp(last[h : h + 1, :]) * grown + contract(faded, v, ((0,), (0,)))
        offset[...] = before + last

    s_copy = pltpu.make_async_remote_copy(
        src_ref=state_out, dst_ref=state_got, send_sem=s_send, recv_sem=s_recv,
        device_id={"seq": lax.rem(place + 1, n_seq)}, device_id_type=MESH)

    @pl.when(place == 0)
    def _():
        enter[...] = jnp.zeros_like(enter)
        state_out[...] = state[...].astype(BF16)
        if n_seq > 1:
            s_copy.start()

    def owner(o):
        t, s = o // 2, o % 2
        return lax.rem(chip + t + 1, chips) * 2 + lax.rem(core + s + (t + 1) // chips, 2)

    def gate_of(step):
        o, r = lax.rem(step, n_mp), step // n_mp
        here = at_rows(owner(o) * parts + r)
        g = jnp.dot(x[here, :], w[3], preferred_element_type=F32).astype(BF16).astype(F32)
        gates[...] = g / (1.0 + jnp.exp(-g))

    weights[3].wait()
    gate_of(0)

    @pl.when(place > 0)
    def _():
        s_copy.wait_recv()
        enter[...] = state_got[...]

    if n_seq > 2:
        @pl.when(jnp.logical_and(place > 0, place < n_seq - 1))
        def _():
            for h in range(heads):
                total = jnp.exp(offset[h : h + 1, 0:1])
                state_out[h] = (total * enter[h].astype(F32) + state[h]).astype(BF16)
            s_copy.start()

    def m_copy(o, r):
        to = owner(o)
        return pltpu.make_async_remote_copy(
            src_ref=moved.at[at_rows(to * parts + r), :], dst_ref=got.at[me, at_rows(r), :],
            send_sem=m_send.at[o, r], recv_sem=m_recv.at[me, r],
            device_id={"mp": to}, device_id_type=MESH)

    def q_copy(o, r):
        to = owner(o)
        return pltpu.make_async_remote_copy(
            src_ref=sq_out.at[to * parts + r], dst_ref=sq_got.at[me, r],
            send_sem=q_send.at[o, r], recv_sem=q_recv.at[me, r],
            device_id={"mp": to}, device_id_type=MESH)

    steps = n_mp * parts
    ones = jnp.ones((8, width), BF16)

    @pl.loop(0, steps)
    def _(step):
        o, r = lax.rem(step, n_mp), step // n_mp
        block = owner(o) * parts + r
        here = at_rows(block)
        squares = jnp.zeros((8, rows), F32)
        for h in range(heads):
            part = slice(h * head_width, (h + 1) * head_width)
            whole = local_out[here, part] + jnp.dot(q_in[here, part], enter[h], preferred_element_type=F32)
            whole = whole.astype(BF16).astype(F32)
            square = whole * whole
            high = square.astype(BF16)
            low = (square - high.astype(F32)).astype(BF16)
            unit = ones[:, part]
            squares += contract(unit, high, ((1,), (1,))) + contract(unit, low, ((1,), (1,)))
            moved[here, part] = (gates[:, part] * whole).astype(BF16)
        sq_out[block] = squares

        @pl.when(o < n_mp - 1)
        def _():
            q_copy(o, r).start()
            m_copy(o, r).start()

        @pl.when(o == n_mp - 1)
        def _():
            got[me, at_rows(r), :] = moved[here, :]
            sq_got[me, r] = squares

        @pl.when(step < steps - 1)
        def _():
            gate_of(step + 1)

    def m_arrival(source, r):
        there = got.at[source, at_rows(r), :]
        return pltpu.make_async_remote_copy(
            src_ref=there, dst_ref=there, send_sem=m_send.at[0, r], recv_sem=m_recv.at[source, r],
            device_id={"mp": partner}, device_id_type=MESH)

    def q_arrival(source, r):
        there = sq_got.at[source, r]
        return pltpu.make_async_remote_copy(
            src_ref=there, dst_ref=there, send_sem=q_send.at[0, r], recv_sem=q_recv.at[source, r],
            device_id={"mp": partner}, device_id_type=MESH)

    for r in range(parts):
        for other in range(1, n_mp):
            source = lax.rem(me + other, n_mp)
            q_arrival(source, r).wait_recv()
            m_arrival(source, r).wait_recv()
        total = sq_got[0, r]
        for source in range(1, n_mp):
            total += sq_got[source, r]
        scale = lax.rsqrt(total * (1.0 / (n_mp * width)) + 1e-06).T[:, 0:1]
        span = slice(r * rows, (r + 1) * rows)
        for source in range(n_mp):
            part = slice(source * width, (source + 1) * width)
            out[span, part] = (got[source, span, :].astype(F32) * scale * gain[:, part]).astype(BF16)

    @pl.loop(0, chunks)
    def _(c):
        for step in range(1, chips):
            y_copy(c, step).wait_send()
        for step in range(chips):
            d_copy(c, step).wait_send()

    @pl.loop(0, n_mp - 1)
    def _(o):
        for r in range(parts):
            q_copy(o, r).wait_send()
            m_copy(o, r).wait_send()

    if n_seq > 1:
        @pl.when(place < n_seq - 1)
        def _():
            s_copy.wait_send()


def body(n_mp, n_seq, tokens, w_query, w_key, w_value, w_gate, decay_exponent, forget, norm_gain):
    seq_rows, width = tokens.shape
    features = w_query.shape[0]
    heads = decay_exponent.shape[0]
    own_rows = seq_rows // n_mp
    rows = 256 if own_rows % 256 == 0 else own_rows
    chunks, parts = seq_rows // rows, own_rows // rows
    rate = jnp.log1p(-jnp.exp2(-decay_exponent.astype(F32)))
    lanes = -(-heads // 8) * 8
    decay = jnp.pad((rate[None, :] - forget).T, ((0, lanes - heads), (0, 0)))
    hbm, vmem = pl.BlockSpec(memory_space=pl.ANY), pl.BlockSpec(memory_space=pltpu.VMEM)
    dma = pltpu.SemaphoreType.DMA
    chips = n_mp // 2
    return pl.pallas_call(
        functools.partial(kernel, n_mp, n_seq, heads, rows),
        out_shape=jax.ShapeDtypeStruct((own_rows, features), BF16),
        in_specs=[hbm] * 5 + [vmem] * 2,
        out_specs=vmem,
        scratch_shapes=[
            pltpu.VMEM((seq_rows, features), BF16),
            pltpu.VMEM((4, features, width), BF16),
            pltpu.VMEM((seq_rows, width), F32),
            pltpu.VMEM((seq_rows, width), BF16),
            pltpu.VMEM((seq_rows, width), BF16),
            pltpu.VMEM((n_mp, own_rows, width), BF16),
            pltpu.VMEM((chunks, 8, rows), F32),
            pltpu.VMEM((n_mp, parts, 8, rows), F32),
            pltpu.VMEM((rows, width), F32),
            pltpu.VMEM((heads, DH, DH), F32),
            pltpu.VMEM((heads, DH, DH), BF16),
            pltpu.VMEM((heads, DH, DH), BF16),
            pltpu.VMEM((heads, DH, DH), BF16),
            pltpu.VMEM((lanes, 128), F32),
            dma((4,)),
            dma((chunks,)),
            dma((chunks, chips)),
            dma((chunks, chips)),
            dma((chunks, chips)),
            dma((chunks, chips)),
            dma,
            dma,
            dma((n_mp, parts)),
            dma((n_mp, parts)),
            dma((n_mp, parts)),
            dma((n_mp, parts)),
        ],
        compiler_params=pltpu.CompilerParams(
            collective_id=0, has_side_effects=True, vmem_limit_bytes=60 * 1024 * 1024
        ),
    )(tokens, w_query, w_key, w_value, w_gate, decay, norm_gain[None, :])


def solution(mesh):
    placed = (
        P(("dp", "seq"), "mp"),
        P(None, "mp"),
        P(None, "mp"),
        P(None, "mp"),
        P(None, "mp"),
        P("mp"),
        P(("dp", "seq"), "mp"),
        P(),
    )
    return jax.shard_map(
        functools.partial(body, mesh.shape["mp"], mesh.shape["seq"]),
        mesh=mesh,
        in_specs=placed,
        out_specs=P(("dp", "seq", "mp"), None),
        check_vma=False,
    )
```

time: 341 us -> 91.4 us (0.27); the launches traced: 336 us -> 91.1 us
  local copies, waits for them, and re-layouts: 131 us -> 3.8 us
  Pallas kernels: 0 us -> 85.8 us
  waiting for transfers between devices: 78.7 us -> 0 us
  matrix products: 67.6 us -> 0 us
  other arithmetic: 25.2 us -> 1.5 us
  between operations: 14.1 us -> 0.01 us
  starting transfers between devices: 9.83 us -> 0 us
  blocking collectives: 9.15 us -> 0 us
    dynamic_update_slice x8 -> x0, local copies, waits for them, and re-layouts: 88.5 us -> none  [run_blocks(): lax.scan(advance, initial, (shaped(queries), shaped(key_rows), shaped(val...]
    pallas_call x0 -> x1, Pallas kernels: none -> 85.8 us  [body(): pl.pallas_call(functools.partial(kernel, n_mp, n_seq, heads, rows), out_s...]
    dot_general x17 -> x0, matrix products: 67.6 us -> none  [the longest x4 35.9 us: body(): results.append(jnp.dot(piece, weight, preferred_element_type=jnp.float32))]
    all_gather x1 -> x0, waiting for transfers between devices: 58 us -> none  [body(): piece = lax.all_gather(tokens, 'mp', axis=1, tiled=True)]
    all_to_all x2 -> x0, waiting for transfers between devices: 20 us -> none  [the longest x1 20 us: body(): lax.all_to_all(output, 'mp', split_axis=0, concat_axis=1, tiled=True)]
    reshape x8 -> x0, local copies, waits for them, and re-layouts: 14.2 us -> none  [the longest x3 8.09 us: shaped(): return source.reshape(block_count, block_rows, head_count, head_width)]
    dynamic_slice x8 -> x0, local copies, waits for them, and re-layouts: 11.9 us -> none  [run_blocks(): lax.scan(advance, initial, (shaped(queries), shaped(key_rows), shaped(val...]
    all_to_all x2 -> x0, starting transfers between devices: 9.83 us -> none  [the longest x1 5.17 us: body(): lax.all_to_all(output, 'mp', split_axis=0, concat_axis=1, tiled=True)]
  transfers between devices with their start and end apart: 3 -> 0, of which waited for: 2 -> 0; matrix products, arithmetic and copies ran while one was open for 7% -> 0% of each run, Pallas kernels for 0% -> 0%
where the time goes in v1:
time: 91.4 us; the launch traced here: 91.1 us
  Pallas kernels  85.8 us (94%)
  local copies, waits for them, and re-layouts  3.8 us (4%)
  other arithmetic  1.5 us (2%)
    pallas_call x1, Pallas kernels, body(): pl.pallas_call(functools.partial(kernel, n_mp, n_seq, heads, rows), out_s...  85.8 us
    unnamed x1, local copies, waits for them, and re-layouts  3.16 us

profile of v1, /device:TPU:11, one launch (start us, length us, event | category | flops | bytes accessed | tf_op | source)
XLA Modules:
  0.0 91.1 jit_solution(6599683773083354401)
XLA Ops:
  0.0 0.7 negate_log-plus-one_fusion
  0.7 0.8 subtract_bitcast_fusion
  1.5 0.6 pad.4.decay
  2.1 85.8 %shard_map.82 = bf16[512,2048]{1,0:T(8,128)(2,1)} custom-call(bf16[2048,512]{1,0:T(8,128)(2,1)} %tokens.1, bf16[2048,512]{1,0:T(8,128)(2,1)} %wq.1, bf16[2048,512]{1,0:T(8,128)(2,1)} %wk.1, bf16[2048,512]{1,0:T(8,128)(2,1)} %wv.1, bf16[2048,512]{1,0:T(8,128)(2,1)} %wg.1, f32[8,2048]{1,0:T(8,128)} %pad.4.decay, f32[1,2048]{1,0:T(1,128)} %bitcast.3), custom_call_target="tpu_custom_call" | custom-call | tf_op jit(solution)/shard_map/pallas_call | solution.py:293
  88.0 3.2 %copy.10 = bf16[512,2048]{1,0:T(8,128)(2,1)} copy(bf16[512,2048]{1,0:T(8,128)(2,1)} %shard_map.82) | data formatting | bytes 4194304

commit v2 on v1

--- a/solution.py
+++ b/solution.py
@@ -19,8 +19,8 @@
 
 def kernel(
     n_mp, n_seq, heads, rows,
-    tokens, wq, wk, wv, wg, decay, gain, out,
-    x, w, local_out, q_in, moved, got, sq_out, sq_got, gates, state, enter, state_out, state_got, offset,
+    tokens, wq, wk, wv, wg, forget, rate, gain, out,
+    x, w, local_out, q_in, moved, got, sq_out, sq_got, gates, state, held, enter, state_out, state_got, offset,
     weight_sem, own_sem, y_send, y_recv, d_send, d_recv, s_send, s_recv, m_send, m_recv, q_send, q_recv,
 ):
     me = lax.axis_index("mp")
@@ -113,6 +113,11 @@
     earlier = lax.broadcasted_iota(jnp.int32, (rows, rows), 1)
     causal = later >= earlier
     summing = (later <= earlier).astype(F32)
+    exact = lax.Precision.HIGHEST
+
+    s_copy = pltpu.make_async_remote_copy(
+        src_ref=state_out, dst_ref=state_got, send_sem=s_send, recv_sem=s_recv,
+        device_id={"seq": lax.rem(place + 1, n_seq)}, device_id_type=MESH)
 
     @pl.loop(0, chunks)
     def _(c):
@@ -121,41 +126,48 @@
             y_arrival(c, step).wait_recv()
             d_copy(c, step).start()
         own_copy(c).wait()
-        running = jnp.dot(decay[:, here], summing, precision=lax.Precision.HIGHEST, preferred_element_type=F32)
-        by_row = running.T
+        decay = rate[...] - forget[:, here]
+        running = jnp.dot(decay, summing, precision=exact, preferred_element_type=F32)
+        by_row = lax.dot_general(
+            causal.astype(F32), decay, (((1,), (1,)), ((), ())), precision=exact, preferred_element_type=F32)
         last = running[:, rows - 1 :]
         before = offset[...]
         for step in range(chips):
             d_arrival(c, step).wait_recv()
         piece = x[here, :]
-        query = jnp.dot(piece, w[0], preferred_element_type=F32).astype(BF16)
         key = (jnp.dot(piece, w[1], preferred_element_type=F32) * DH ** (-0.5)).astype(BF16)
         value = jnp.dot(piece, w[2], preferred_element_type=F32).astype(BF16)
+        for h in range(heads):
+            part = slice(h * head_width, (h + 1) * head_width)
+            k, v = key[:, part], value[:, part]
+            end = last[h : h + 1, :]
+            grown = state[h]
+            held[h] = grown.astype(BF16)
+            faded = (k.astype(F32) * jnp.exp(end - by_row[:, h : h + 1])).astype(BF16)
+            state[h] = jnp.exp(end) * grown + contract(faded, v, ((0,), (0,)))
+
+        @pl.when(jnp.logical_and(place == 0, c == chunks - 1))
+        def _():
+            state_out[...] = state[...].astype(BF16)
+            if n_seq > 1:
+                s_copy.start()
+
+        query = jnp.dot(piece, w[0], preferred_element_type=F32).astype(BF16)
         for h in range(heads):
             part = slice(h * head_width, (h + 1) * head_width)
             q, k, v = query[:, part], key[:, part], value[:, part]
             col = by_row[:, h : h + 1]
             mask = jnp.exp(jnp.where(causal, col - running[h : h + 1, :], -1e30))
             scores = (contract(q, k, ((1,), (1,))) * mask).astype(BF16)
-            grown = state[h]
             qf = q.astype(F32)
-            carried = jnp.dot((qf * jnp.exp(col)).astype(BF16), grown.astype(BF16), preferred_element_type=F32)
+            carried = jnp.dot((qf * jnp.exp(col)).astype(BF16), held[h], preferred_element_type=F32)
             local_out[here, part] = jnp.dot(scores, v, preferred_element_type=F32) + carried
             q_in[here, part] = (qf * jnp.exp(col + before[h : h + 1, 0:1])).astype(BF16)
-            faded = (k.astype(F32) * jnp.exp(last[h : h + 1, :] - col)).astype(BF16)
-            state[h] = jnp.exp(last[h : h + 1, :]) * grown + contract(faded, v, ((0,), (0,)))
         offset[...] = before + last
-
-    s_copy = pltpu.make_async_remote_copy(
-        src_ref=state_out, dst_ref=state_got, send_sem=s_send, recv_sem=s_recv,
-        device_id={"seq": lax.rem(place + 1, n_seq)}, device_id_type=MESH)
 
     @pl.when(place == 0)
     def _():
         enter[...] = jnp.zeros_like(enter)
-        state_out[...] = state[...].astype(BF16)
-        if n_seq > 1:
-            s_copy.start()
 
     def owner(o):
         t, s = o // 2, o % 2
@@ -205,23 +217,29 @@
         o, r = lax.rem(step, n_mp), step // n_mp
         block = owner(o) * parts + r
         here = at_rows(block)
-        squares = jnp.zeros((8, rows), F32)
+        kept = []
         for h in range(heads):
             part = slice(h * head_width, (h + 1) * head_width)
             whole = local_out[here, part] + jnp.dot(q_in[here, part], enter[h], preferred_element_type=F32)
-            whole = whole.astype(BF16).astype(F32)
-            square = whole * whole
+            kept.append(whole.astype(BF16))
+            moved[here, part] = (gates[:, part] * kept[h].astype(F32)).astype(BF16)
+
+        @pl.when(o < n_mp - 1)
+        def _():
+            m_copy(o, r).start()
+
+        squares = jnp.zeros((8, rows), F32)
+        for h in range(heads):
+            square = kept[h].astype(F32) * kept[h].astype(F32)
             high = square.astype(BF16)
             low = (square - high.astype(F32)).astype(BF16)
-            unit = ones[:, part]
+            unit = ones[:, h * head_width : (h + 1) * head_width]
             squares += contract(unit, high, ((1,), (1,))) + contract(unit, low, ((1,), (1,)))
-            moved[here, part] = (gates[:, part] * whole).astype(BF16)
         sq_out[block] = squares
 
         @pl.when(o < n_mp - 1)
         def _():
             q_copy(o, r).start()
-            m_copy(o, r).start()
 
         @pl.when(o == n_mp - 1)
         def _():
@@ -285,15 +303,13 @@
     rows = 256 if own_rows % 256 == 0 else own_rows
     chunks, parts = seq_rows // rows, own_rows // rows
     rate = jnp.log1p(-jnp.exp2(-decay_exponent.astype(F32)))
-    lanes = -(-heads // 8) * 8
-    decay = jnp.pad((rate[None, :] - forget).T, ((0, lanes - heads), (0, 0)))
     hbm, vmem = pl.BlockSpec(memory_space=pl.ANY), pl.BlockSpec(memory_space=pltpu.VMEM)
     dma = pltpu.SemaphoreType.DMA
     chips = n_mp // 2
     return pl.pallas_call(
         functools.partial(kernel, n_mp, n_seq, heads, rows),
         out_shape=jax.ShapeDtypeStruct((own_rows, features), BF16),
-        in_specs=[hbm] * 5 + [vmem] * 2,
+        in_specs=[hbm] * 5 + [vmem] * 3,
         out_specs=vmem,
         scratch_shapes=[
             pltpu.VMEM((seq_rows, features), BF16),
@@ -309,7 +325,8 @@
             pltpu.VMEM((heads, DH, DH), BF16),
             pltpu.VMEM((heads, DH, DH), BF16),
             pltpu.VMEM((heads, DH, DH), BF16),
-            pltpu.VMEM((lanes, 128), F32),
+            pltpu.VMEM((heads, DH, DH), BF16),
+            pltpu.VMEM((heads, 128), F32),
             dma((4,)),
             dma((chunks,)),
             dma((chunks, chips)),
@@ -326,7 +343,7 @@
         compiler_params=pltpu.CompilerParams(
             collective_id=0, has_side_effects=True, vmem_limit_bytes=60 * 1024 * 1024
         ),
-    )(tokens, w_query, w_key, w_value, w_gate, decay, norm_gain[None, :])
+    )(tokens, w_query, w_key, w_value, w_gate, forget.T, rate[:, None], norm_gain[None, :])
 
 
 def solution(mesh):

time: 91.4 us -> 89.2 us (0.976)
  Pallas kernels: 85.8 us -> 84.5 us
    pallas_call x1, Pallas kernels: 85.8 us -> 84.5 us  [body(): pl.pallas_call(functools.partial(kernel, n_mp, n_seq, heads, rows), out_s...]
where the time goes in v2:
time: 89.2 us; the launch traced here: 89 us
  Pallas kernels  84.5 us (95%)
  local copies, waits for them, and re-layouts  3.83 us (4%)
    pallas_call x1, Pallas kernels, body(): pl.pallas_call(functools.partial(kernel, n_mp, n_seq, heads, rows), out_s...  84.5 us
    unnamed x1, local copies, waits for them, and re-layouts  3.16 us

profile of v2, /device:TPU:11, one launch (start us, length us, event | category | flops | bytes accessed | tf_op | source)
XLA Modules:
  0.0 89.0 jit_solution(18027673448184256589)
XLA Ops:
  0.0 0.7 log-plus-one_bitcast_fusion
  0.7 0.7 copy.9.rate
  1.3 84.5 %shard_map.82 = bf16[512,2048]{1,0:T(8,128)(2,1)} custom-call(bf16[2048,512]{1,0:T(8,128)(2,1)} %tokens.1, bf16[2048,512]{1,0:T(8,128)(2,1)} %wq.1, bf16[2048,512]{1,0:T(8,128)(2,1)} %wk.1, bf16[2048,512]{1,0:T(8,128)(2,1)} %wv.1, bf16[2048,512]{1,0:T(8,128)(2,1)} %wg.1, f32[4,2048]{1,0:T(4,128)} %bitcast.4, f32[4,1]{1,0:T(4,128)} %copy.9.rate, ...), custom_call_target="tpu_custom_call" | custom-call | tf_op jit(solution)/shard_map/pallas_call | solution.py:309
  85.8 3.2 %copy.11 = bf16[512,2048]{1,0:T(8,128)(2,1)} copy(bf16[512,2048]{1,0:T(8,128)(2,1)} %shard_map.82) | data formatting | bytes 4194304
